TPU v7x, 32 devices: a whole 2x2x4 slice. The times are simulated.
32 devices in a mesh: ctx: 8 (over z, y), req: 4 (over x, core).
Axes of the slice: x: 2, y: 2, z: 4, core: 2. Of those that a mesh axis runs over, the one named last changes fastest.
Arguments:
- queries: bfloat16 [4096, 1024], P(('req', 'ctx')), parts along dimension 0, may hold values from -6 to 6
- keys: bfloat16 [4096, 256], P(('req', 'ctx')), parts along dimension 0, may hold values from -6 to 6
- lse: float32 [16, 4096], P(None, ('req', 'ctx')), parts along dimension 1, may hold values from -0.5 to 15, as said below
- length: int32 [4], P('req'), parts along dimension 0, may hold values from 512 to 1024
Outputs:
- key_scores: float32 [16, 4096], P(None, ('req', 'ctx')), parts along dimension 1
There are 4 independent parts, one for each index of `req`. A program takes and returns all parts, laid end to end along the dimension named above; each array names one. Nothing has to cross between parts.
Inputs may be any that keep to these rules, and one draw needn't show every extreme that they name: lse[h, i] is the logarithm of i + 1 plus an offset between -0.5 and 3.
All inputs are finite; a program needn't handle non-finite values.
Results may differ from a plain program's by a relative error of at most 0.0003.
Values may be sent and summed in bfloat16 or wider, within the bound.
No kernel may reach another device: no remote copies, remote signals or barrier semaphores. Data moves between devices by JAX's collectives and lax.ppermute only.
A program may use at most 64 MiB of HBM per device.

v0:
```python
import math
import jax
import jax.numpy as jnp
from jax import lax
from jax.sharding import PartitionSpec as P

HEAD_DIM = 64


def block_terms(query_set, lse_set, positions, key_block, key_start, limit):
    heads = lse_set.shape[0]
    rows_here = query_set.shape[0]
    width = key_block.shape[0]
    kv_heads = key_block.shape[1] // HEAD_DIM
    grouped = query_set.reshape(rows_here, kv_heads, heads // kv_heads, HEAD_DIM)
    key_view = key_block.reshape(width, kv_heads, HEAD_DIM)
    logits = jnp.einsum("rhgd,chd->hgrc", grouped, key_view, preferred_element_type=jnp.float32)
    logits = logits.reshape(heads, rows_here, width) * HEAD_DIM ** (-0.5)
    key_pos = key_start + jnp.arange(width, dtype=jnp.int32)
    valid = (positions[:, None] >= key_pos[None, :]) & (positions[:, None] < limit)
    weights = jnp.where(valid[None], jnp.exp(logits - lse_set[:, :, None]), jnp.float32(0.0))
    return jnp.sum(weights, axis=1)


def make_absorb(query_sets, limit, heads, total, piece, start):
    width = piece.shape[0]
    step_len = math.gcd(width, 512)
    turns = width // step_len

    def skipped(*operands):
        return jnp.zeros((heads, step_len), jnp.float32)

    def one_turn(turn, running):
        offset = turn * step_len
        key_block = lax.dynamic_slice_in_dim(piece, offset, step_len, 0)
        key_start = start + offset
        part_sum = jnp.zeros((heads, step_len), jnp.float32)
        for query_set, lse_set, positions in query_sets:
            needed = (key_start <= jnp.max(positions)) & (key_start < limit)
            part_sum = lax.cond(
                needed,
                block_terms,
                skipped,
                query_set,
                lse_set,
                positions,
                key_block,
                key_start,
                limit,
            )
        current = lax.dynamic_slice(running, (0, key_start), (heads, step_len))
        return lax.dynamic_update_slice(running, current + part_sum, (0, key_start))

    return lax.fori_loop(0, turns, one_turn, total)


def shards(queries, keys, lse, length):
    tok_rows = queries.shape[0]
    heads = lse.shape[0]
    devices_ctx = lax.axis_size("ctx")
    my_index = lax.axis_index("ctx")
    limit = length[0]
    first_row = my_index * tok_rows
    query_sets = [(queries, lse, first_row + jnp.arange(tok_rows, dtype=jnp.int32))]
    empty = jnp.zeros((heads, tok_rows * devices_ctx), jnp.float32)
    totals = make_absorb(
        query_sets,
        limit,
        heads,
        empty,
        lax.all_gather(keys, "ctx", axis=0, tiled=True),
        jnp.int32(0),
    )
    return lax.psum_scatter(totals, "ctx", scatter_dimension=1, tiled=True)


def solution(mesh):
    placed = (P(("req", "ctx"), None), P(("req", "ctx"), None), P(None, ("req", "ctx")), P("req"))
    return jax.shard_map(
        shards, mesh=mesh, in_specs=placed, out_specs=P(None, ("req", "ctx")), check_vma=False
    )
```

profile of v0, /device:TPU:0, one launch (start us, length us, event | category | flops | bytes accessed | tf_op | source)
XLA Modules:
  0.0 107.6 jit_solution(11371074071570174559)
XLA Ops:
  6.5 0.0 reduce-scatter.2.cloned.1.call-start
  6.5 0.7 add_reduce_fusion
  7.2 0.9 copy.5
  8.2 0.0 copy-start.1
  8.2 1.1 %copy.6 = bf16[128,1024]{0,1:T(8,128)(2,1)S(1)} copy(bf16[128,1024]{1,0:T(8,128)(2,1)} %param.8) | data formatting | bytes 524288
  9.3 29.6 %all_gather.3 = bf16[1024,256]{0,1:T(8,128)(2,1)S(1)} all-gather(bf16[128,256]{0,1:T(8,128)(2,1)S(1)} %copy.5), channel_id=1, replica_groups=mesh['ctx'=8,'req'=4] {'ctx'}, dimensions={0}, use_global_device_ids=true | all-gather | bytes 589824 | tf_op jit(solution)/shard_map/all_gather | solution.py:71
  38.9 0.0 copy-done.1
  38.9 4.9 %while.15 = (s32[]{:T(128)}, f32[16,1024]{1,0:T(8,128)S(1)}, s32[]{:T(128)}, s32[]{:T(128)}, bf16[1024,256]{0,1:T(8,128)(2,1)S(1)}, /*index=5*/bf16[128,1024]{0,...) while((s32[]{:T(128)}, f32[16,1024]{1,0:T(8,128)S(1)}, ...), condition=%wide.region_5.6_spmd.clone, body=%wide.region_1.5_spmd.clone.sunk | while | flops 138543888 | bytes 1391129 | solution.py:54
  40.2 2.2 %conditional.3 = (f32[16,512]{1,0:T(8,128)S(1)}) conditional(s32[]{:T(128)} %convert_element_type.10, () %tuple.49, (s32[]{:T(128)}, s32[]{:T(128)}, s32[]{:T(128)}, bf16[1024,256]{0,1:T(8,128)(2,1)S(1)}, s32[]{:T(128)}, /*index=5*/bf16[128,1024]{0,1:T(8,128)(2,1)S(1)}, f32[16,128]{1,0:T(8,128)S(1)}, s32[128]{0:T(128)S(1)}) %tuple.50), branch_computations={%region_2.0_spmd, %region_3.4_spmd} | conditional | flops 138535680 | bytes 1292056 | solution.py:40
  40.2 0.7 broadcast_compare_fusion
  40.9 0.1 compare_and_fusion
  41.0 1.4 %fusion.4 = f32[4,4,512]{2,1,0:T(4,128)S(1)} fusion(bf16[512,4,64,1]{0,2,3,1:T(8,128)(2,1)S(1)} %bitcast.18, bf16[128,4,4,64]{0,3,2,1:T(8,128)(2,1)S(1)} %bitcast.19, f32[4,4,128]{2,1,0:T(4,128)S(1)} %bitcast.20, pred[128,512]{1,0:T(8,128)(4,1)S(1)} %compare_and_fusion), kind=kOutput, calls=%fused_computation.4 | convolution fusion | flops 138403840 | bytes 630784 | tf_op jit(solution)/shard_map/while/body/eval_jaxpr/cond/branch_1_fun/rhgd,chd->hgrc/dot_general | solution.py:17
  43.8 0.0 copy-start
  43.8 0.6 copy-done
  44.4 0.0 reduce-scatter.2.cloned.1.call-update
  44.5 56.3 %reduce-scatter.2.cloned.1.call-done = f32[16,128]{1,0:T(8,128)} async-done(((f32[16,1024]{1,0:T(8,128)}), f32[16,128]{1,0:T(8,128)}) %reduce-scatter.2.cloned.1.call-update) | async-done | bytes 8208 | tf_op jit(solution)/shard_map/reduce_scatter | solution.py:74
  (10 shorter events, 0.1 us)
Async XLA Ops:
  6.5 94.3 %reduce-scatter.2.cloned.1.call-start = ((), (), s32[]{:S(2)}) async-start(), calls=%async_computation.1 | async-start | bytes 73728 | tf_op jit(solution)/shard_map/reduce_scatter | solution.py:74
  8.2 30.7 %copy-start.1 = (f32[16,128]{1,0:T(8,128)S(1)}, f32[16,128]{1,0:T(8,128)}, u32[]{:S(2)}) copy-start(f32[16,128]{1,0:T(8,128)} %param.10) | copy-start | bytes 24580
  43.8 0.6 copy-start
Sparse Core Ops, SparseCore 0:
  44.6 56.1 reduce-scatter.1
where the time goes:
time: 108 us
  waiting for transfers between devices  56.3 us (52%)
  blocking collectives  29.6 us (27%)
  between operations  13.4 us (12%)
  local copies, waits for them, and re-layouts  2.75 us (3%)
  loops' own time  2.73 us (3%)
  other arithmetic  1.46 us (1%)
  matrix products  1.35 us (1%)
    reduce_scatter x1, waiting for transfers between devices, shards(): return lax.psum_scatter(totals, 'ctx', scatter_dimension=1, tiled=True)  56.3 us
    all_gather x1, blocking collectives, shards(): lax.all_gather(keys, 'ctx', axis=0, tiled=True)  29.6 us
    unnamed x6, local copies, waits for them, and re-layouts  2.69 us
    another operation x1, loops' own time, make_absorb(): return lax.fori_loop(0, turns, one_turn, total)  2.66 us
  transfers between devices with their start and end apart: 1, of which 1 were waited for; matrix products, arithmetic and copies ran while one was open for 0% of the time, Pallas kernels for 0%

commit v1 on v0

--- a/solution.py
+++ b/solution.py
@@ -5,6 +5,11 @@
 from jax.sharding import PartitionSpec as P
 
 HEAD_DIM = 64
+
+
+def swapped_in(x, mesh_axis, along):
+    repeated = jnp.stack([x] * lax.axis_size(mesh_axis))
+    return jnp.concatenate(lax.all_to_all(repeated, mesh_axis, 0, 0), axis=along)
 
 
 def block_terms(query_set, lse_set, positions, key_block, key_start, limit):
@@ -63,14 +68,7 @@
     first_row = my_index * tok_rows
     query_sets = [(queries, lse, first_row + jnp.arange(tok_rows, dtype=jnp.int32))]
     empty = jnp.zeros((heads, tok_rows * devices_ctx), jnp.float32)
-    totals = make_absorb(
-        query_sets,
-        limit,
-        heads,
-        empty,
-        lax.all_gather(keys, "ctx", axis=0, tiled=True),
-        jnp.int32(0),
-    )
+    totals = make_absorb(query_sets, limit, heads, empty, swapped_in(keys, "ctx", 0), jnp.int32(0))
     return lax.psum_scatter(totals, "ctx", scatter_dimension=1, tiled=True)
 
 

time: 108 us -> 100 us (0.926)
  blocking collectives: 29.6 us -> 0 us
  waiting for transfers between devices: 56.3 us -> 69.7 us
  starting transfers between devices: 0.01 us -> 7.48 us
    all_gather x1 -> x0, blocking collectives: 29.6 us -> none  [shards(): lax.all_gather(keys, 'ctx', axis=0, tiled=True)]
    all_to_all x0 -> x1, waiting for transfers between devices: none -> 13.6 us  [swapped_in(): lax.all_to_all(repeated, mesh_axis, 0, 0)]
    all_to_all x0 -> x1, starting transfers between devices: none -> 7.44 us  [swapped_in(): lax.all_to_all(repeated, mesh_axis, 0, 0)]
    unnamed x6 -> x9, local copies, waits for them, and re-layouts: 2.69 us -> 2.4 us
  transfers between devices with their start and end apart: 1 -> 2, of which waited for: 1 -> 2; matrix products, arithmetic and copies ran while one was open for 0% -> 1% of each run, Pallas kernels for 0% -> 0%
where the time goes in v1:
time: 100 us; the launch traced here: 99.8 us
  waiting for transfers between devices  69.7 us (70%)
  between operations  13.5 us (14%)
  starting transfers between devices  7.48 us (7%)
  local copies, waits for them, and re-layouts  3.53 us (4%)
  loops' own time  2.79 us (3%)
  other arithmetic  1.49 us (1%)
  matrix products  1.34 us (1%)
    reduce_scatter x1, waiting for transfers between devices, shards(): return lax.psum_scatter(totals, 'ctx', scatter_dimension=1, tiled=True)  56.1 us
    all_to_all x1, waiting for transfers between devices, swapped_in(): lax.all_to_all(repeated, mesh_axis, 0, 0)  13.6 us
    all_to_all x1, starting transfers between devices, swapped_in(): lax.all_to_all(repeated, mesh_axis, 0, 0)  7.44 us
    another operation x1, loops' own time, make_absorb(): return lax.fori_loop(0, turns, one_turn, total)  2.71 us
    unnamed x9, local copies, waits for them, and re-layouts  2.4 us
  transfers between devices with their start and end apart: 2, of which 2 were waited for; matrix products, arithmetic and copies ran while one was open for 1% of the time, Pallas kernels for 0%

profile of v1, /device:TPU:0, one launch (start us, length us, event | category | flops | bytes accessed | tf_op | source)
XLA Modules:
  0.0 99.8 jit_solution(1489892444329969358)
XLA Ops:
  6.5 0.9 copy.9
  7.5 0.9 stack.2
  8.4 0.0 copy-start.1
  8.4 7.4 %all-to-all-start = ((bf16[8,128,256]{1,2,0:T(8,128)(2,1)}), bf16[8,128,256]{1,2,0:T(8,128)(2,1)S(1)}, u32[]{:S(2)}, u32[]{:S(2)}) async-start(bf16[8,128,256]{1,2,0:T(8,128)(2,1)} %stack.2), calls=%async_computation | async-start | bytes 1048576 | tf_op jit(solution)/shard_map/all_to_all | solution.py:12
  15.8 0.0 reduce-scatter.2.cloned.1.call-start
  15.8 0.7 add_reduce_fusion
  16.5 0.0 copy-done.1
  16.5 0.2 copy.12
  16.7 13.6 %all-to-all-done = bf16[8,128,256]{1,2,0:T(8,128)(2,1)S(1)} async-done(((bf16[8,128,256]{1,2,0:T(8,128)(2,1)}), bf16[8,128,256]{1,2,0:T(8,128)(2,1)S(1)}, u32[]{:S(2)}, u32[]{:S(2)}) %all-to-all-start) | async-done | bytes 524320 | tf_op jit(solution)/shard_map/all_to_all | solution.py:12
  30.3 0.2 copy.10
  30.5 0.0 copy-start.2
  30.5 0.2 copy.11
  30.7 0.5 copy-done.2
  31.2 5.0 %while.15 = (s32[]{:T(128)}, f32[16,1024]{1,0:T(8,128)S(1)}, s32[]{:T(128)}, s32[]{:T(128)}, bf16[1024,256]{0,1:T(8,128)(2,1)S(1)}, /*index=5*/bf16[128,1024]{0,...) while((s32[]{:T(128)}, f32[16,1024]{1,0:T(8,128)S(1)}, ...), condition=%wide.region_5.6_spmd.clone, body=%wide.region_1.5_spmd.clone.sunk | while | flops 138543888 | bytes 1391129 | solution.py:59
  32.5 2.2 %conditional.3 = (f32[16,512]{1,0:T(8,128)S(1)}) conditional(s32[]{:T(128)} %convert_element_type.10, () %tuple.51, (s32[]{:T(128)}, s32[]{:T(128)}, s32[]{:T(128)}, bf16[1024,256]{0,1:T(8,128)(2,1)S(1)}, s32[]{:T(128)}, /*index=5*/bf16[128,1024]{0,1:T(8,128)(2,1)S(1)}, f32[16,128]{1,0:T(8,128)S(1)}, s32[128]{0:T(128)S(1)}) %tuple.52), branch_computations={%region_2.0_spmd, %region_3.4_spmd} | conditional | flops 138535680 | bytes 1292056 | solution.py:45
  32.6 0.7 broadcast_compare_fusion
  33.2 0.1 compare_and_fusion
  33.4 1.3 %fusion.4 = f32[4,4,512]{2,1,0:T(4,128)S(1)} fusion(bf16[512,4,64,1]{0,2,3,1:T(8,128)(2,1)S(1)} %bitcast.19, bf16[128,4,4,64]{0,3,2,1:T(8,128)(2,1)S(1)} %bitcast.21, f32[4,4,128]{2,1,0:T(4,128)S(1)} %bitcast.22, pred[128,512]{1,0:T(8,128)(4,1)S(1)} %compare_and_fusion), kind=kOutput, calls=%fused_computation.4 | convolution fusion | flops 138403840 | bytes 630784 | tf_op jit(solution)/shard_map/while/body/eval_jaxpr/cond/branch_1_fun/rhgd,chd->hgrc/dot_general | solution.py:22
  36.2 0.0 copy-start
  36.2 0.6 copy-done
  36.8 0.0 reduce-scatter.2.cloned.1.call-update
  36.8 56.1 %reduce-scatter.2.cloned.1.call-done = f32[16,128]{1,0:T(8,128)} async-done(((f32[16,1024]{1,0:T(8,128)}), f32[16,128]{1,0:T(8,128)}) %reduce-scatter.2.cloned.1.call-update) | async-done | bytes 8208 | tf_op jit(solution)/shard_map/reduce_scatter | solution.py:72
  (10 shorter events, 0.1 us)
Async XLA Ops:
  8.4 8.2 %copy-start.1 = (bf16[128,1024]{1,0:T(8,128)(2,1)S(1)}, bf16[128,1024]{1,0:T(8,128)(2,1)}, u32[]{:S(2)}) copy-start(bf16[128,1024]{1,0:T(8,128)(2,1)} %param.8) | copy-start | bytes 786436
  8.4 21.9 %all-to-all-start = ((bf16[8,128,256]{1,2,0:T(8,128)(2,1)}), bf16[8,128,256]{1,2,0:T(8,128)(2,1)S(1)}, u32[]{:S(2)}, u32[]{:S(2)}) async-start(bf16[8,128,256]{1,2,0:T(8,128)(2,1)} %stack.2), calls=%async_computation | async-start | bytes 1048576 | tf_op jit(solution)/shard_map/all_to_all | solution.py:12
  15.8 77.2 %reduce-scatter.2.cloned.1.call-start = ((), (), s32[]{:S(2)}) async-start(), calls=%async_computation.2 | async-start | bytes 73728 | tf_op jit(solution)/shard_map/reduce_scatter | solution.py:72
  30.5 0.7 copy-start.2
  36.2 0.6 copy-start
Sparse Core Ops, SparseCore 0:
  37.0 55.9 reduce-scatter.1
